TPU v7x, 8 devices: a whole 2x2x1 slice. The times are simulated.
8 devices in a mesh: dp: 1 (over z), ep2: 2 (over y), ep: 4 (over x, core).
Axes of the slice: x: 2, y: 2, z: 1, core: 2. Of those that a mesh axis runs over, the one named last changes fastest.
Arguments:
- tokens: bfloat16 [1024, 2048], P(('dp', 'ep2', 'ep'))
- expert_ids: int32 [1024, 8], P(('dp', 'ep2', 'ep'))
- gates: float32 [1024, 8], P(('dp', 'ep2', 'ep'))
- w_gate: bfloat16 [128, 2048, 768], P(('ep2', 'ep'))
- w_up: bfloat16 [128, 2048, 768], P(('ep2', 'ep'))
- w_down: bfloat16 [128, 768, 2048], P(('ep2', 'ep'))
Outputs:
- output: bfloat16 [1024, 2048], P(('dp', 'ep2', 'ep'))
All inputs are finite; a program needn't handle non-finite values.
Results may differ from a plain program's by a relative error of at most 0.0011.
Values are sent between devices in bfloat16 or wider.
A program may use at most 1 GiB of HBM per device.

v0:
```python
import jax
import jax.numpy as jnp
from jax import lax
from jax.sharding import PartitionSpec as P


def slot_matrix(expert_ids, n_expert, row_cap):
    n_tok, n_top = expert_ids.shape
    flat_ids = expert_ids.reshape(n_tok * n_top)
    expert_hot = (flat_ids[:, None] == jnp.arange(n_expert)[None, :]).astype(jnp.int32)
    running = jnp.cumsum(expert_hot, axis=0)
    slot_pos = jnp.sum(expert_hot * running, axis=1) - 1
    dest_pos = flat_ids * row_cap + slot_pos
    slot_hot = dest_pos[:, None] == jnp.arange(n_expert * row_cap)[None, :]
    return slot_hot.reshape(n_tok, n_top, n_expert * row_cap).astype(jnp.bfloat16)


def expert_ffn(rows_in, w_gate, w_up, w_down):
    act_gate = jnp.einsum('slcd,ldf->slcf', rows_in, w_gate, preferred_element_type=jnp.float32)
    act_up = jnp.einsum('slcd,ldf->slcf', rows_in, w_up, preferred_element_type=jnp.float32)
    hidden = (jax.nn.silu(act_gate) * act_up).astype(jnp.bfloat16)
    return jnp.einsum('slcf,lfd->slcd', hidden, w_down, preferred_element_type=jnp.float32).astype(jnp.bfloat16)


def solution(mesh):
    group_axes = ('ep2', 'ep')
    n_group = mesh.shape['ep2'] * mesh.shape['ep']
    row_spec = P(('dp', 'ep2', 'ep'), None)
    weight_spec = P(group_axes, None, None)

    def device_step(tokens, expert_ids, gates, w_gate, w_up, w_down):
        n_tok, n_top = expert_ids.shape
        local_count, model_dim = w_gate.shape[0], w_gate.shape[1]
        n_expert = local_count * n_group
        row_cap = -(-(n_tok * n_top) // n_expert)
        slot_hot = slot_matrix(expert_ids, n_expert, row_cap)
        send_buf = jnp.einsum('tjp,td->pd', slot_hot, tokens, preferred_element_type=jnp.float32).astype(jnp.bfloat16)
        recv_buf = lax.all_to_all(send_buf, group_axes, 0, 0, tiled=True)
        expert_out = expert_ffn(recv_buf.reshape(n_group, local_count, row_cap, model_dim), w_gate, w_up, w_down)
        back_buf = lax.all_to_all(expert_out.reshape(n_expert * row_cap, model_dim), group_axes, 0, 0, tiled=True)
        picked = jnp.einsum('tjp,pd->tjd', slot_hot, back_buf, preferred_element_type=jnp.float32)
        total = tokens.astype(jnp.float32)
        for slot_j in range(n_top):
            total = total + gates[:, slot_j:slot_j + 1] * picked[:, slot_j]
        return total.astype(jnp.bfloat16)

    return jax.shard_map(device_step, mesh=mesh, in_specs=(row_spec, row_spec, row_spec, weight_spec, weight_spec, weight_spec), out_specs=row_spec, check_vma=False)
```

profile of v0, /device:TPU:0, one launch (start us, length us, event | category | flops | bytes accessed | tf_op | source)
XLA Modules:
  0.0 186.0 jit_solution(7938774993304556541)
XLA Ops:
  0.0 0.8 copy.27
  0.8 0.1 eq.64
  0.9 0.1 eq.60
  1.0 0.1 copy.29
  1.1 0.2 fusion.45
  1.4 0.1 copy.30
  1.5 0.4 fusion.44
  1.9 0.1 sub.7
  2.1 0.7 multiply_add_fusion
  2.8 0.1 copy.32
  2.9 1.3 convert_reduce_fusion
  4.2 0.0 copy-done
  4.2 1.3 fusion.49
  5.5 53.1 %all_to_all.21 = bf16[8,128,2048]{2,1,0:T(8,128)(2,1)} all-to-all(bf16[8,128,2048]{2,1,0:T(8,128)(2,1)S(1)} %bitcast.168), channel_id=1, replica_groups=mesh['dp'=1,'ep2'=2,'ep'=4] {'ep2','ep'}, dimensions={0} | all-to-all | bytes 8388608 | tf_op jit(solution)/shard_map/all_to_all | solution.py:38
  58.6 19.8 %fusion.2 = f32[16,8,8,768]{3,2,1,0:T(8,128)S(1)} fusion(bf16[16,2048,768]{2,1,0:T(8,128)(2,1)} %param.10, bf16[8,128,2048]{2,1,0:T(8,128)(2,1)} %all_to_all.21), kind=kOutput, calls=%fused_computation.2 | convolution fusion | flops 3221225472 | bytes 57671680 | tf_op jit(solution)/shard_map/slcd,ldf->slcf/dot_general | solution.py:20
  78.4 21.0 %fusion.14.clone.4 = bf16[8,16,8,768]{3,2,0,1:T(8,128)(2,1)} fusion(f32[16,8,8,768]{3,2,1,0:T(8,128)S(1)} %fusion.2, bf16[16,2048,768]{2,1,0:T(8,128)(2,1)} %param.9, bf16[8,128,2048]{2,1,0:T(8,128)(2,1)} %all_to_all.21), kind=kOutput, calls=%fused_computation.18.clone.clone.clone.1 | convolution fusion | flops 3225944064 | bytes 59244544 | tf_op jit(solution)/shard_map/slcd,ldf->slcf/dot_general | solution.py:19
  99.4 21.4 %convert_bitcast_fusion = bf16[8,16,8,2048]{3,2,0,1:T(8,128)(2,1)} fusion(bf16[16,768,2048]{2,1,0:T(8,128)(2,1)} %param.11, bf16[8,16,8,768]{3,2,0,1:T(8,128)(2,1)} %fusion.14.clone.4), kind=kOutput, calls=%fused_computation.7 | convolution fusion | flops 3223322624 | bytes 56098816 | tf_op jit(solution)/shard_map/slcf,lfd->slcd/dot_general | solution.py:22
  120.9 4.7 %copy.51 = bf16[8,16,8,2048]{3,2,1,0:T(8,128)(2,1)} copy(bf16[8,16,8,2048]{3,2,0,1:T(8,128)(2,1)} %convert_bitcast_fusion) | data formatting | bytes 8388608 | tf_op jit(solution)/shard_map/convert_element_type | solution.py:22
  125.6 3.6 %all-to-all-start.1 = ((bf16[8,128,2048]{2,1,0:T(8,128)(2,1)}), bf16[8,128,2048]{2,1,0:T(8,128)(2,1)}, u32[]{:S(2)}, u32[]{:S(2)}) async-start(bf16[8,128,2048]{2,1,0:T(8,128)(2,1)} %bitcast.169), calls=%async_computation.1 | async-start | bytes 8388608 | tf_op jit(solution)/shard_map/all_to_all | solution.py:40
  129.2 0.0 copy-done.2
  129.2 48.8 %all-to-all-done.1 = bf16[8,128,2048]{2,1,0:T(8,128)(2,1)} async-done(((bf16[8,128,2048]{2,1,0:T(8,128)(2,1)}), bf16[8,128,2048]{2,1,0:T(8,128)(2,1)}, u32[]{:S(2)}, u32[]{:S(2)}) %all-to-all-start.1) | async-done | bytes 4194336 | tf_op jit(solution)/shard_map/all_to_all | solution.py:40
  178.0 6.4 %fusion.7 = f32[128,8,2048]{2,0,1:T(8,128)S(1)} fusion(bf16[1024,2048,1]{1,0,2:T(8,128)(2,1)} %bitcast.18, s32[128,8]{0,1:T(8,128)S(1)} %multiply_add_fusion), kind=kOutput, calls=%fused_computation.12 | convolution fusion | flops 4296015872 | bytes 12587008 | tf_op jit(solution)/shard_map/tjp,pd->tjd/dot_general | solution.py:41
  184.5 0.0 copy-done.1
  184.5 1.5 fusion.25
  (10 shorter events, 0.1 us)
Async XLA Ops:
  0.0 4.2 %copy-start = (bf16[128,2048]{1,0:T(8,128)(2,1)S(1)}, bf16[128,2048]{1,0:T(8,128)(2,1)}, u32[]{:S(2)}) copy-start(bf16[128,2048]{1,0:T(8,128)(2,1)} %param.6) | copy-start | bytes 1572868
  125.6 3.6 %copy-start.2 = (f32[128,8]{0,1:T(8,128)S(1)}, f32[128,8]{0,1:T(8,128)}, u32[]{:S(2)}) copy-start(f32[128,8]{0,1:T(8,128)} %param.8) | copy-start | bytes 12292
  125.6 52.4 %all-to-all-start.1 = ((bf16[8,128,2048]{2,1,0:T(8,128)(2,1)}), bf16[8,128,2048]{2,1,0:T(8,128)(2,1)}, u32[]{:S(2)}, u32[]{:S(2)}) async-start(bf16[8,128,2048]{2,1,0:T(8,128)(2,1)} %bitcast.169), calls=%async_computation.1 | async-start | bytes 8388608 | tf_op jit(solution)/shard_map/all_to_all | solution.py:40
  178.0 6.4 %copy-start.1 = (bf16[128,2048]{1,0:T(8,128)(2,1)S(1)}, bf16[128,2048]{1,0:T(8,128)(2,1)}, u32[]{:S(2)}) copy-start(bf16[128,2048]{1,0:T(8,128)(2,1)} %param.6) | copy-start | bytes 1572868
where the time goes:
time: 186 us
  matrix products  69.9 us (38%)
  blocking collectives  53.1 us (29%)
  waiting for transfers between devices  48.8 us (26%)
  local copies, waits for them, and re-layouts  6.23 us (3%)
  other arithmetic  4.18 us (2%)
  starting transfers between devices  3.59 us (2%)
    all_to_all x1, blocking collectives, device_step(): recv_buf = lax.all_to_all(send_buf, group_axes, 0, 0, tiled=True)  53.1 us
    all_to_all x1, waiting for transfers between devices, device_step(): lax.all_to_all(expert_out.reshape(n_expert * row_cap, model_dim), group_a...  48.8 us
    dot_general x1, matrix products, expert_ffn(): jnp.einsum('slcf,lfd->slcd', hidden, w_down, preferred_element_type=jnp.f...  21.4 us
    dot_general x1, matrix products, expert_ffn(): jnp.einsum('slcd,ldf->slcf', rows_in, w_gate, preferred_element_type=jnp....  21 us
    dot_general x1, matrix products, expert_ffn(): jnp.einsum('slcd,ldf->slcf', rows_in, w_up, preferred_element_type=jnp.fl...  19.8 us
    dot_general x1, matrix products, device_step(): jnp.einsum('tjp,pd->tjd', slot_hot, back_buf, preferred_element_type=jnp....  6.44 us
    convert_element_type x1, local copies, waits for them, and re-layouts, expert_ffn(): jnp.einsum('slcf,lfd->slcd', hidden, w_down, preferred_element_type=jnp.f...  4.74 us
  transfers between devices with their start and end apart: 1, of which 1 were waited for; matrix products, arithmetic and copies ran while one was open for 0% of the time, Pallas kernels for 0%

commit v1 on v0

v1 whole, which is shorter than its diff:
```python
import functools

import jax
import jax.numpy as jnp
from jax import lax
from jax.experimental import pallas as pl
from jax.experimental.pallas import tpu as pltpu
from jax.sharding import PartitionSpec as P

N_DEV = 8
N_TOK = 128
N_TOP = 8
DIM = 2048
FFN = 768
N_EXP = 128
N_LOC = 16
CAP = 8
RING = 5
CHUNKS = 4
CHUNK_ROWS = N_TOK // CHUNKS
N_PAIR = N_LOC // 2
BF16 = jnp.bfloat16
F32 = jnp.float32

OFFSETS = ((1, 1, 0), (1, 1, 1), (1, 0, 0), (0, 1, 0), (1, 0, 1), (0, 1, 1), (0, 0, 1))


def iota(shape, axis):
    return lax.broadcasted_iota(jnp.int32, shape, axis)


def dot(a, b):
    return jnp.dot(a, b, preferred_element_type=F32)


def moe_kernel(tok, ids_t, ids, gates, w1, w3, w2, out,
               xall, xg, yrecv, acc, pm, gm, w1b, w3b, w2b, idsall,
               sem_w, sem_tok, ids_send, ids_recv, ag_send, ag_recv, y_send, y_recv):
    dp = lax.axis_index('dp')
    gy = lax.axis_index('ep2')
    ep = lax.axis_index('ep')
    gx, gc = ep // 2, ep % 2
    me = gy * 4 + ep

    def flip(v, d):
        return v + d * (1 - 2 * v)

    def index_of(off):
        dx, dy, dc = off
        return flip(gy, dy) * 4 + flip(gx, dx) * 2 + flip(gc, dc)

    def mesh_id(idx):
        return (dp, idx // 4, idx % 4)

    def weight_copy(e, which):
        slot = e % RING
        source, ring = ((w1, w1b), (w3, w3b), (w2, w2b))[which]
        return pltpu.make_async_copy(source.at[e], ring.at[slot], sem_w.at[which, slot])

    tok_copy = pltpu.make_async_copy(tok, xall.at[me], sem_tok)
    tok_copy.start()
    for e in range(RING):
        for which in range(3):
            weight_copy(e, which).start()

    barrier = pltpu.get_barrier_semaphore()
    for off in OFFSETS:
        pl.semaphore_signal(barrier, inc=1, device_id=mesh_id(index_of(off)),
                            device_id_type=pl.DeviceIdType.MESH)
    pl.semaphore_wait(barrier, len(OFFSETS))

    def ids_copy(r, owner, dest):
        return pltpu.make_async_remote_copy(
            src_ref=ids_t, dst_ref=idsall.at[owner], send_sem=ids_send.at[r], recv_sem=ids_recv.at[r],
            device_id=mesh_id(dest), device_id_type=pl.DeviceIdType.MESH)

    for r, off in enumerate(OFFSETS):
        ids_copy(r, me, index_of(off)).start()

    partner = index_of((0, 0, 1))
    x_next = index_of((1, 0, 0))
    y_next = index_of((0, 1, 0))
    diag = index_of((1, 1, 0))
    relay_from = x_next + gc * (y_next - x_next)
    relay_to = y_next + gc * (x_next - y_next)

    def tok_send(shard, q, kind, dest):
        rows = pl.ds(q * CHUNK_ROWS, CHUNK_ROWS)
        return pltpu.make_async_remote_copy(
            src_ref=xall.at[shard, rows], dst_ref=xall.at[shard, rows],
            send_sem=ag_send.at[kind, q], recv_sem=ag_recv.at[shard, q],
            device_id=mesh_id(dest), device_id_type=pl.DeviceIdType.MESH)

    tok_copy.wait()
    for q in range(CHUNKS):
        tok_send(me, q, 1, x_next).start()
        tok_send(me, q, 2, y_next).start()
    for q in range(CHUNKS):
        tok_send(me, q, 0, partner).start()

    acc[...] = xall[me].astype(F32)
    idsall[me] = ids_t[...]

    gate_exp = jnp.zeros((N_TOK, N_EXP), F32)
    hot = jnp.zeros((N_TOK, N_EXP), F32)
    lane = iota((N_TOK, N_EXP), 1)
    for j in range(N_TOP):
        same = ids[:, j:j + 1] == lane
        gate_exp = gate_exp + jnp.where(same, gates[:, j:j + 1], 0.0)
        hot = hot + jnp.where(same, 1.0, 0.0)
    low = (iota((N_TOK, N_TOK), 1) < iota((N_TOK, N_TOK), 0)).astype(F32).astype(BF16)
    rank = dot(low, hot.astype(BF16))
    slot_of = jnp.where(hot > 0.5, rank, -1.0)
    g1 = gate_exp.astype(BF16)
    rest = gate_exp - g1.astype(F32)
    g2 = rest.astype(BF16)
    g3 = (rest - g2.astype(F32)).astype(BF16)
    stacked = jnp.concatenate([slot_of.astype(BF16), g1, g2, g3], axis=0)
    for p in range(N_PAIR):
        col = iota((N_EXP, N_TOK), 1)
        expert = (col // 16) * N_LOC + 2 * p + (col // 8) % 2
        spread = (iota((N_EXP, N_TOK), 0) == expert).astype(F32).astype(BF16)
        wide = dot(stacked, spread)
        keep = wide[:N_TOK] == (iota((N_TOK, N_TOK), 1) % CAP).astype(F32)
        for part in range(3):
            piece = wide[(part + 1) * N_TOK:(part + 2) * N_TOK]
            gm[part, :, p * N_TOK:(p + 1) * N_TOK] = jnp.where(keep, piece, 0.0).astype(BF16)

    for r, off in enumerate(OFFSETS):
        ids_copy(r, index_of(off), index_of(off)).wait_recv()
    expert_row = me * N_LOC + iota((N_LOC, N_TOK), 0)
    hots = []
    for s in range(N_DEV):
        any_hit = jnp.zeros((N_LOC, N_TOK), F32)
        for j in range(N_TOP):
            any_hit = any_hit + jnp.where(idsall[s, j:j + 1, :] == expert_row, 1.0, 0.0)
        hots.append(any_hit)
    hot_t = jnp.concatenate(hots, axis=0)
    up = (iota((N_TOK, N_TOK), 0) < iota((N_TOK, N_TOK), 1)).astype(F32).astype(BF16)
    slot_t = jnp.where(hot_t > 0.5, dot(hot_t.astype(BF16), up), -1.0).astype(BF16)
    for k in range(4):
        row = iota((256, N_TOK), 0)
        source = 2 * k + (row // 8) % 2
        spread = (iota((256, N_TOK), 1) == source * N_LOC + row // 16).astype(F32).astype(BF16)
        wide = dot(spread, slot_t)
        one = jnp.where(wide == (row % CAP).astype(F32), 1.0, 0.0)
        left = jnp.where((row // 8) % 2 == 0, one, 0.0)
        right = one - left
        pm[k, :, :N_TOK] = left.astype(BF16)
        pm[k, :, N_TOK:] = right.astype(BF16)

    def gather(chip):
        rows = xall[pl.ds(chip * 2, 2)].reshape(2 * N_TOK, DIM)
        for n in range(0, DIM, 512):
            xg[chip, :, n:n + 512] = dot(pm[chip], rows[:, n:n + 512]).astype(BF16)

    def wait_tok(shard, q):
        tok_send(shard, q, 0, partner).wait_recv()

    for q in range(CHUNKS):
        wait_tok(relay_from, q)
        tok_send(relay_from, q, 4, relay_to).start()
        tok_send(relay_from, q, 3, partner).start()
        wait_tok(relay_to, q)
        tok_send(relay_to, q, 5, partner).start()
        if q == 1:
            for qq in range(CHUNKS):
                wait_tok(partner, qq)
            gather(me // 2)
    for q in range(CHUNKS):
        wait_tok(diag, q)
        tok_send(diag, q, 6, partner).start()
        if q == 0:
            for qq in range(CHUNKS):
                wait_tok(index_of((1, 0, 1)), qq)
                wait_tok(index_of((0, 1, 1)), qq)
            gather(x_next // 2)
            gather(y_next // 2)
    for q in range(CHUNKS):
        wait_tok(index_of((1, 1, 1)), q)
    gather(diag // 2)

    for q in range(CHUNKS):
        tok_send(me, q, 0, partner).wait_send()
        tok_send(me, q, 1, x_next).wait_send()
        tok_send(me, q, 2, y_next).wait_send()
        tok_send(relay_from, q, 3, partner).wait_send()
        tok_send(relay_from, q, 4, relay_to).wait_send()
        tok_send(relay_to, q, 5, partner).wait_send()
        tok_send(diag, q, 6, partner).wait_send()
    for r, off in enumerate(OFFSETS):
        ids_copy(r, me, index_of(off)).wait_send()

    def y_copy(p, r, owner, dest):
        return pltpu.make_async_remote_copy(
            src_ref=xall.at[p, pl.ds(dest * 16, 16)], dst_ref=yrecv.at[p, pl.ds(owner * 16, 16)],
            send_sem=y_send.at[p, r], recv_sem=y_recv.at[p, r],
            device_id=mesh_id(dest), device_id_type=pl.DeviceIdType.MESH)

    def refill(e, which):
        @pl.when(e + RING < N_LOC)
        def _():
            weight_copy(e + RING, which).start()

    def pair_step(p, _):
        hidden = []
        for half in range(2):
            e = 2 * p + half
            slot = e % RING
            rows = jnp.concatenate(
                [xg[k, pl.ds(pl.multiple_of(e * 16, 16), 16), :] for k in range(4)], axis=0)
            weight_copy(e, 0).wait()
            act_gate = dot(rows, w1b[slot])
            refill(e, 0)
            weight_copy(e, 1).wait()
            act_up = dot(rows, w3b[slot])
            refill(e, 1)
            hidden.append((act_gate * jax.nn.sigmoid(act_gate) * act_up).astype(BF16))
        for half in range(2):
            weight_copy(2 * p + half, 2).wait()
        for n in range(0, DIM, 512):
            parts = []
            for half in range(2):
                slot = (2 * p + half) % RING
                parts.append(dot(hidden[half], w2b[slot, :, n:n + 512]).reshape(N_DEV, CAP, 512))
            both = jnp.concatenate(parts, axis=1).reshape(N_TOK, 512)
            xall[p, :, n:n + 512] = both.astype(BF16)
        for half in range(2):
            refill(2 * p + half, 2)
        mine = pl.ds(pl.multiple_of(me * 16, 16), 16)
        yrecv[p, mine, :] = xall[p, mine, :]
        for r, off in enumerate(OFFSETS):
            y_copy(p, r, me, index_of(off)).start()
        return 0

    lax.fori_loop(0, N_PAIR, pair_step, 0)

    def combine(h, _):
        for r, off in enumerate(OFFSETS):
            y_copy(2 * h, r, index_of(off), index_of(off)).wait_recv()
            y_copy(2 * h + 1, r, index_of(off), index_of(off)).wait_recv()
        cols = pl.ds(pl.multiple_of(h * 256, 256), 256)
        for n in range(0, DIM, 512):
            rows = yrecv[pl.ds(2 * h, 2), :, n:n + 512].reshape(256, 512)
            total = dot(gm[0, :, cols], rows) + dot(gm[1, :, cols], rows) + dot(gm[2, :, cols], rows)
            acc[:, n:n + 512] += total
        return 0

    lax.fori_loop(0, N_PAIR // 2, combine, 0)
    out[...] = acc[...].astype(BF16)

    def drain(p, _):
        for r, off in enumerate(OFFSETS):
            y_copy(p, r, me, index_of(off)).wait_send()
        return 0

    lax.fori_loop(0, N_PAIR, drain, 0)


def solution(mesh):
    group_axes = ('ep2', 'ep')
    row_spec = P(('dp', 'ep2', 'ep'), None)
    weight_spec = P(group_axes, None, None)

    def device_step(tokens, expert_ids, gates, w_gate, w_up, w_down):
        vmem = pl.BlockSpec(memory_space=pltpu.VMEM)
        hbm = pl.BlockSpec(memory_space=pl.ANY)
        dma = pltpu.SemaphoreType.DMA
        return pl.pallas_call(
            moe_kernel,
            out_shape=jax.ShapeDtypeStruct((N_TOK, DIM), BF16),
            in_specs=[hbm, vmem, vmem, vmem, hbm, hbm, hbm],
            out_specs=vmem,
            scratch_shapes=[
                pltpu.VMEM((N_DEV, N_TOK, DIM), BF16),
                pltpu.VMEM((4, 256, DIM), BF16),
                pltpu.VMEM((N_PAIR, N_TOK, DIM), BF16),
                pltpu.VMEM((N_TOK, DIM), F32),
                pltpu.VMEM((4, 256, 256), BF16),
                pltpu.VMEM((3, N_TOK, N_EXP * CAP), BF16),
                pltpu.VMEM((RING, DIM, FFN), BF16),
                pltpu.VMEM((RING, DIM, FFN), BF16),
                pltpu.VMEM((RING, FFN, DIM), BF16),
                pltpu.VMEM((N_DEV, N_TOP, N_TOK), jnp.int32),
                dma((3, RING)),
                dma,
                dma((7,)),
                dma((7,)),
                dma((7, CHUNKS)),
                dma((N_DEV, CHUNKS)),
                dma((N_PAIR, 7)),
                dma((N_PAIR, 7)),
            ],
            compiler_params=pltpu.CompilerParams(
                collective_id=0, has_side_effects=True, vmem_limit_bytes=67043328),
            name='moe_step',
        )(tokens, expert_ids.T, expert_ids, gates, w_gate, w_up, w_down)

    return jax.shard_map(device_step, mesh=mesh,
                         in_specs=(row_spec, row_spec, row_spec, weight_spec, weight_spec, weight_spec),
                         out_specs=row_spec, check_vma=False)
```

time: 186 us -> 98.1 us (0.53)
  Pallas kernels: 0 us -> 93.1 us
  matrix products: 69.9 us -> 0 us
  blocking collectives: 53.1 us -> 0 us
  waiting for transfers between devices: 48.8 us -> 0 us
  other arithmetic: 4.18 us -> 0 us
  starting transfers between devices: 3.59 us -> 0 us
    pallas_call x0 -> x1, Pallas kernels: none -> 93.1 us  [device_step(): pl.pallas_call(moe_kernel, out_shape=jax.ShapeDtypeStruct((N_TOK, DIM), B...]
    dot_general x5 -> x0, matrix products: 69.9 us -> none  [the longest x1 21.4 us: expert_ffn(): jnp.einsum('slcf,lfd->slcd', hidden, w_down, preferred_element_type=jnp.f...]
    all_to_all x1 -> x0, blocking collectives: 53.1 us -> none  [device_step(): recv_buf = lax.all_to_all(send_buf, group_axes, 0, 0, tiled=True)]
    all_to_all x1 -> x0, waiting for transfers between devices: 48.8 us -> none  [device_step(): lax.all_to_all(expert_out.reshape(n_expert * row_cap, model_dim), group_a...]
    convert_element_type x1 -> x0, local copies, waits for them, and re-layouts: 4.74 us -> none  [expert_ffn(): jnp.einsum('slcf,lfd->slcd', hidden, w_down, preferred_element_type=jnp.f...]
    unnamed x7 -> x3, local copies, waits for them, and re-layouts: 0.86 us -> 4.7 us
    all_to_all x1 -> x0, starting transfers between devices: 3.59 us -> none  [device_step(): lax.all_to_all(expert_out.reshape(n_expert * row_cap, model_dim), group_a...]
  transfers between devices with their start and end apart: 1 -> 0, of which waited for: 1 -> 0; matrix products, arithmetic and copies ran while one was open for 0% -> 0% of each run, Pallas kernels for 0% -> 0%
where the time goes in v1:
time: 98.1 us; the launch traced here: 97.8 us
  Pallas kernels  93.1 us (95%)
  local copies, waits for them, and re-layouts  4.7 us (5%)
    pallas_call x1, Pallas kernels, device_step(): pl.pallas_call(moe_kernel, out_shape=jax.ShapeDtypeStruct((N_TOK, DIM), B...  93.1 us
    unnamed x3, local copies, waits for them, and re-layouts  4.7 us

profile of v1, /device:TPU:0, one launch (start us, length us, event | category | flops | bytes accessed | tf_op | source)
XLA Modules:
  0.0 97.8 jit_solution(11918573595150886410)
XLA Ops:
  0.0 1.4 %copy.8.gates = f32[128,8]{1,0:T(8,128)} copy(f32[128,8]{0,1:T(8,128)} %param.8) | data formatting | bytes 8192 | tf_op args[2]
  1.4 1.4 %copy.7.ids = s32[128,8]{1,0:T(8,128)} copy(s32[128,8]{0,1:T(8,128)} %param.7) | data formatting | bytes 8192 | tf_op args[1]
  2.8 93.1 %moe_step.1 = bf16[128,2048]{1,0:T(8,128)(2,1)} custom-call(bf16[128,2048]{1,0:T(8,128)(2,1)} %tok.1, s32[8,128]{1,0:T(8,128)} %bitcast.1, s32[128,8]{1,0:T(8,128)} %copy.7.ids, f32[128,8]{1,0:T(8,128)} %copy.8.gates, bf16[16,2048,768]{2,1,0:T(8,128)(2,1)} %w1.1, bf16[16,2048,768]{2,1,0:T(8,128)(2,1)} %w3.1, bf16[16,768,2048]{2,1,0:T(8,128)(2,1)} %w2.1), custom_call_target="tpu_custom_call" | custom-call | tf_op jit(solution)/shard_map/moe_step/pallas_call | solution.py:269
  95.9 1.9 %copy.10 = bf16[128,2048]{1,0:T(8,128)(2,1)} copy(bf16[128,2048]{1,0:T(8,128)(2,1)} %moe_step.1) | data formatting | bytes 1048576
